TPU v7x, 32 devices: a whole 2x2x4 slice. The times are simulated.
32 devices in a mesh: parts: 2 (over y), gz: 8 (over z, x), gy: 2 (over core).
Axes of the slice: x: 2, y: 2, z: 4, core: 2. Of those that a mesh axis runs over, the one named last changes fastest.
Arguments:
- direction: float32 [3, 16, 128, 128], P(None, ('parts', 'gz'), 'gy'), parts along dimension 1, may hold values from -6 to 6
- region: int32 [16, 128, 128], P(('parts', 'gz'), 'gy'), parts along dimension 0, may hold values from 0 to 3
- saturation: float32 [3], replicated, may hold values from 0.5 to 2
- kernel_main: float32 [6, 16, 256, 128], P(None, 'gz', 'gy'), may hold values from -6 to 6
- kernel_nyq: float32 [6, 16, 256], P(None, 'gz', 'gy'), may hold values from -6 to 6
Outputs:
- field: float32 [3, 16, 128, 128], P(None, ('parts', 'gz'), 'gy'), parts along dimension 1
There are 2 independent parts, one for each index of `parts`. A program takes and returns all parts, laid end to end along the dimension named above; an argument that names none is the same for every part. Nothing has to cross between parts.
Inputs may be any that keep to these rules, and one draw needn't show every extreme that they name: `region`: 0 marks an empty cell; other ids name materials.
All inputs are finite; a program needn't handle non-finite values.
Results may differ from a plain program's by a relative error of at most 0.00007.
Values sent between devices are 32-bit elements; how exact they have to be, the bound alone decides.
A program may use at most 64 MiB of HBM per device.

v0:
```python
import math
import jax
import jax.numpy as jnp
from jax import lax
from jax.sharding import PartitionSpec as P

exchange_stiffness = 0.25
tensor_index = ((0, 3, 4), (3, 1, 5), (4, 5, 2))
highest = lax.Precision.HIGHEST


def with_halo(cells, sides, width):
    for axis, dim in sides:
        count = lax.axis_size(axis)
        ends = count - 1
        head = lax.slice_in_dim(cells, 0, width, axis=dim)
        tail = lax.slice_in_dim(cells, cells.shape[dim] - width, cells.shape[dim], axis=dim)
        cells = jnp.concatenate(
            [
                lax.ppermute(tail, axis, [(i, (i + 1) % count) for i in range(ends)]),
                cells,
                lax.ppermute(head, axis, [((i + 1) % count, i) for i in range(ends)]),
            ],
            axis=dim,
        )
    return cells


def phase(first, second, period):
    product = first[:, None] * second[None, :] % period
    angle = 2.0 * math.pi / period * product.astype(jnp.float32)
    return (jnp.cos(angle), jnp.sin(angle))


def slot_frequency(slot_index, bit_count):
    device = slot_index // 2
    reversed_bits = jnp.zeros_like(device)
    for b in range(bit_count):
        reversed_bits = reversed_bits + device // 2**b % 2 * 2 ** (bit_count - 1 - b)
    return 2 * reversed_bits + slot_index % 2


def row_transform(plane):
    columns = plane.shape[2]
    row_count = plane.shape[1]
    positions = jnp.arange(columns, dtype=jnp.int32)
    cosine, sine = phase(positions, positions, 2 * columns)
    table = jnp.concatenate([cosine, -sine], axis=1)
    flat = plane.reshape(3 * row_count, columns)
    both = jnp.dot(flat, table, precision=highest).reshape(3, row_count, 2, columns)
    signs = 1.0 - 2.0 * (positions % 2).astype(jnp.float32)
    nyquist = jnp.dot(flat, signs, precision=highest).reshape(3, row_count)
    return (both[:, :, 0], both[:, :, 1], nyquist)


def column_transform(real_rows, imag_rows, nyquist, cosine, sine):
    new_real = jnp.einsum("kr,crx->ckx", cosine, real_rows, precision=highest) + jnp.einsum(
        "kr,crx->ckx", sine, imag_rows, precision=highest
    )
    new_imag = jnp.einsum("kr,crx->ckx", cosine, imag_rows, precision=highest) - jnp.einsum(
        "kr,crx->ckx", sine, real_rows, precision=highest
    )
    nyq_real = jnp.einsum("kr,cr->ck", cosine, nyquist, precision=highest)
    nyq_imag = -jnp.einsum("kr,cr->ck", sine, nyquist, precision=highest)
    return (jnp.stack([new_real, new_imag], axis=1), jnp.stack([nyq_real, nyq_imag], axis=1))


def plane_transform(values, cosine, sine, direction_sign):
    real_part = values[:, 0]
    imag_part = values[:, 1]
    new_real = jnp.einsum(
        "pz,cz...->cp...", cosine, real_part, precision=highest
    ) - direction_sign * jnp.einsum("pz,cz...->cp...", sine, imag_part, precision=highest)
    new_imag = jnp.einsum(
        "pz,cz...->cp...", cosine, imag_part, precision=highest
    ) + direction_sign * jnp.einsum("pz,cz...->cp...", sine, real_part, precision=highest)
    return jnp.stack([new_real, new_imag], axis=1)


def apply_kernel(spectra, kernel):
    pieces = []
    for i in range(3):
        summed = kernel[tensor_index[i][0]] * spectra[0]
        for j in (1, 2):
            summed = summed + kernel[tensor_index[i][j]] * spectra[j]
        pieces.append(summed)
    return jnp.stack(pieces)


def local(direction, region, saturation, kernel_main, kernel_nyq):
    columns = direction.shape[3]
    own_rows = direction.shape[2]
    groups_y = lax.axis_size("gy")
    groups_z = lax.axis_size("gz")
    bit_count = groups_z.bit_length() - 1
    rows_total = own_rows * groups_y
    period_y = 2 * rows_total
    period_z = 2 * groups_z
    period_x = 2 * columns
    spec_rows = period_y // groups_y
    y_index = lax.axis_index("gy")
    magnetic = (region > 0).astype(jnp.float32)
    strength = jnp.zeros(region.shape, jnp.float32)
    for r in range(saturation.shape[0]):
        strength = strength + jnp.where(region == r + 1, saturation[r], 0.0)
    magnet_plane = (direction * strength[None])[:, 0]
    gathered = lax.all_gather(magnet_plane, "gy", axis=1, tiled=True)
    frequency = y_index * spec_rows + jnp.arange(spec_rows, dtype=jnp.int32)
    cosine, sine = phase(frequency, jnp.arange(rows_total, dtype=jnp.int32), period_y)
    real_rows, imag_rows, nyquist = row_transform(gathered)
    spec_main, spec_nyq = column_transform(real_rows, imag_rows, nyquist, cosine, sine)
    slot_freq = slot_frequency(jnp.arange(period_z, dtype=jnp.int32), bit_count)
    plane_ids = jnp.arange(groups_z, dtype=jnp.int32)
    sent_main, sent_nyq = (
        lax.all_to_all(spec_main[:, :, None], "gz", split_axis=3, concat_axis=2, tiled=True),
        lax.all_to_all(spec_nyq[:, :, None], "gz", split_axis=3, concat_axis=2, tiled=True),
    )
    cosine, sine = phase(slot_freq, plane_ids, period_z)
    done_main = plane_transform(sent_main, cosine, sine, -1.0)
    done_nyq = plane_transform(sent_nyq, cosine, sine, -1.0)
    full_main, full_nyq = (
        lax.all_to_all(done_main, "gz", split_axis=2, concat_axis=3, tiled=True),
        lax.all_to_all(done_nyq, "gz", split_axis=2, concat_axis=3, tiled=True),
    )
    field_main = apply_kernel(full_main, kernel_main)
    field_nyq = apply_kernel(full_nyq, kernel_nyq)
    out_main, out_nyq = (
        lax.all_to_all(field_main, "gz", split_axis=3, concat_axis=2, tiled=True),
        lax.all_to_all(field_nyq, "gz", split_axis=3, concat_axis=2, tiled=True),
    )
    cosine, sine = phase(plane_ids, slot_freq, period_z)
    back_main = plane_transform(out_main, cosine, sine, 1.0)
    back_nyq = plane_transform(out_nyq, cosine, sine, 1.0)
    plane_main, plane_nyq = (
        lax.all_to_all(back_main, "gz", split_axis=2, concat_axis=3, tiled=True),
        lax.all_to_all(back_nyq, "gz", split_axis=2, concat_axis=3, tiled=True),
    )
    plane_main = plane_main[:, :, 0]
    plane_nyq = plane_nyq[:, :, 0]
    frequency = y_index * spec_rows + jnp.arange(spec_rows, dtype=jnp.int32)
    cosine, sine = phase(jnp.arange(rows_total, dtype=jnp.int32), frequency, period_y)
    term_real = jnp.einsum("yk,ckx->cyx", cosine, plane_main[:, 0], precision=highest) - jnp.einsum(
        "yk,ckx->cyx", sine, plane_main[:, 1], precision=highest
    )
    term_imag = jnp.einsum("yk,ckx->cyx", cosine, plane_main[:, 1], precision=highest) + jnp.einsum(
        "yk,ckx->cyx", sine, plane_main[:, 0], precision=highest
    )
    nyq_real = jnp.einsum("yk,ck->cy", cosine, plane_nyq[:, 0], precision=highest) - jnp.einsum(
        "yk,ck->cy", sine, plane_nyq[:, 1], precision=highest
    )
    nyq_imag = jnp.einsum("yk,ck->cy", cosine, plane_nyq[:, 1], precision=highest) + jnp.einsum(
        "yk,ck->cy", sine, plane_nyq[:, 0], precision=highest
    )
    rows_main, rows_nyq = (
        lax.psum_scatter(
            jnp.stack([term_real, term_imag], axis=1), "gy", scatter_dimension=2, tiled=True
        ),
        lax.psum_scatter(
            jnp.stack([nyq_real, nyq_imag], axis=1), "gy", scatter_dimension=2, tiled=True
        ),
    )
    positions = jnp.arange(columns, dtype=jnp.int32)
    cosine, sine = phase(positions, positions, period_x)
    weights = jnp.where(positions == 0, 1.0, 2.0).astype(jnp.float32)[:, None]
    table = jnp.concatenate([weights * cosine, -weights * sine], axis=0)
    flat = jnp.concatenate([rows_main[:, 0], rows_main[:, 1]], axis=2).reshape(
        3 * own_rows, 2 * columns
    )
    signs = 1.0 - 2.0 * (positions % 2).astype(jnp.float32)
    demag = jnp.dot(flat, table, precision=highest).reshape(3, own_rows, columns)
    demag = demag + rows_nyq[:, 0][:, :, None] * signs[None, None, :]
    demag = demag * (1.0 / (period_x * period_y * period_z))
    moment = direction * magnetic[None]
    stacked = jnp.concatenate([moment, magnetic[None]], axis=0)
    rim = with_halo(stacked, (("gz", 1), ("gy", 2)), 1)
    centre = rim[:, 1:2, 1:-1]
    near = rim[:, 0:1, 1:-1] + rim[:, 2:3, 1:-1] + rim[:, 1:2, :-2] + rim[:, 1:2, 2:]
    padded_x = jnp.pad(centre, ((0, 0), (0, 0), (0, 0), (1, 1)))
    near = near + padded_x[..., :-2] + padded_x[..., 2:]
    exchange = exchange_stiffness * magnetic[None] * (near[:3] - near[3:4] * direction)
    return demag[:, None] + exchange


def solution(mesh):
    placed = (
        P(None, ("parts", "gz"), "gy", None),
        P(("parts", "gz"), "gy", None),
        P(),
        P(None, "gz", "gy", None),
        P(None, "gz", "gy"),
    )
    return jax.shard_map(
        local,
        mesh=mesh,
        in_specs=placed,
        out_specs=P(None, ("parts", "gz"), "gy", None),
        check_vma=False,
    )
```

profile of v0, /device:TPU:0, one launch (start us, length us, event | category | flops | bytes accessed | tf_op | source)
XLA Modules:
  0.0 176.9 jit_solution(13148347249901439266)
XLA Ops:
  6.5 0.6 copy-done.4
  7.2 0.6 fusion.308
  7.8 0.8 broadcast_multiply_fusion.2
  8.7 0.7 copy-done.2
  9.4 1.9 %add_bitcast_fusion = f32[64,128]{1,0:T(8,128)S(1)} fusion(s32[1,64,128]{2,1,0:T(8,128)S(1)} %copy-done.2, f32[]{:T(128)} %bitcast.4, f32[]{:T(128)} %bitcast.3, f32[]{:T(128)} %bitcast.2), kind=kLoop, calls=%fused_computation.163 | loop fusion | flops 65536 | bytes 65548 | tf_op jit(solution)/shard_map/mul | solution.py:106
  11.3 2.1 %all-gather = f32[3,1,128,128]{3,2,0,1:T(8,128)S(1)} all-gather(f32[3,1,64,128]{3,2,0,1:T(8,128)S(1)} %get-tuple-element.28), channel_id=2, replica_groups=mesh['parts'=2,'gz'=8,'gy'=2] {'gy'}, dimensions={2}, use_global_device_ids=true | all-gather | bytes 294912 | tf_op jit(solution)/shard_map/all_gather | solution.py:107
  13.7 0.5 convolution_bitcast_fusion
  14.2 0.5 fusion.20
  14.8 0.8 copy.150
  15.6 7.1 %all-to-all-start.4 = ((f32[3,2,1,128]{0,1,2,3:T(2,128)}), f32[3,2,1,128]{0,1,2,3:T(2,128)S(1)}, u32[]{:S(2)}, u32[]{:S(2)}) async-start(f32[3,2,1,128]{0,1,2,3:T(2,128)} %copy.150), calls=%async_computation.4 | async-start | bytes 262144 | tf_op jit(solution)/shard_map/all_to_all | solution.py:116
  23.2 0.5 fusion.32
  23.6 0.7 fusion.36
  24.3 0.7 fusion.37
  25.0 0.7 fusion.7
  25.7 0.7 fusion.6
  26.4 3.7 %all-to-all-done.4 = f32[3,2,1,128]{0,1,2,3:T(2,128)S(1)} async-done(((f32[3,2,1,128]{0,1,2,3:T(2,128)}), f32[3,2,1,128]{0,1,2,3:T(2,128)S(1)}, u32[]{:S(2)}, u32[]{:S(2)}) %all-to-all-start.4) | async-done | bytes 3104 | tf_op jit(solution)/shard_map/all_to_all | solution.py:116
  31.5 0.7 reshape.497
  32.2 3.3 %all-to-all-start.5 = ((f32[8,1,192]{2,1,0:T(1,128)}), f32[8,1,192]{2,1,0:T(1,128)S(1)}, u32[]{:S(2)}, u32[]{:S(2)}) async-start(f32[8,1,192]{2,1,0:T(1,128)} %reshape.497), calls=%async_computation.5 | async-start | bytes 16384 | tf_op jit(solution)/shard_map/all_to_all | solution.py:123
  35.6 0.9 copy.131
  36.5 5.5 %all-to-all-done.5 = f32[8,1,192]{2,1,0:T(1,128)S(1)} async-done(((f32[8,1,192]{2,1,0:T(1,128)}), f32[8,1,192]{2,1,0:T(1,128)S(1)}, u32[]{:S(2)}, u32[]{:S(2)}) %all-to-all-start.5) | async-done | bytes 6176 | tf_op jit(solution)/shard_map/all_to_all | solution.py:123
  42.0 3.5 %all-to-all-start = ((f32[3,2,1,128,128]{4,1,2,0,3:T(2,128)}), f32[3,2,1,128,128]{4,1,2,0,3:T(2,128)S(1)}, u32[]{:S(2)}, u32[]{:S(2)}) async-start(f32[3,2,1,128,128]{4,1,2,0,3:T(2,128)} %copy.131), calls=%async_computation | async-start | bytes 786432 | tf_op jit(solution)/shard_map/all_to_all | solution.py:115
  45.5 0.5 broadcast.794
  46.0 0.6 reduce
  47.2 1.0 reshape.499
  48.2 7.0 %all-to-all-done = f32[3,2,1,128,128]{4,1,2,0,3:T(2,128)S(1)} async-done(((f32[3,2,1,128,128]{4,1,2,0,3:T(2,128)}), f32[3,2,1,128,128]{4,1,2,0,3:T(2,128)S(1)}, u32[]{:S(2)}, u32[]{:S(2)}) %all-to-all-start) | async-done | bytes 393248 | tf_op jit(solution)/shard_map/all_to_all | solution.py:115
  55.2 3.7 %all-to-all-start.6 = ((f32[8,1,192]{2,1,0:T(1,128)}), f32[8,1,192]{2,1,0:T(1,128)S(1)}, u32[]{:S(2)}, u32[]{:S(2)}) async-start(f32[8,1,192]{2,1,0:T(1,128)} %reshape.499), calls=%async_computation.6 | async-start | bytes 16384 | tf_op jit(solution)/shard_map/all_to_all | solution.py:129
  58.9 0.6 convolution_multiply_fusion.1
  59.5 0.6 convolution_multiply_fusion
  60.1 0.6 fusion.1
  60.7 0.6 fusion
  61.3 1.1 copy.135
  62.4 2.9 %all-to-all-done.6 = f32[8,1,192]{2,1,0:T(1,128)S(1)} async-done(((f32[8,1,192]{2,1,0:T(1,128)}), f32[8,1,192]{2,1,0:T(1,128)S(1)}, u32[]{:S(2)}, u32[]{:S(2)}) %all-to-all-start.6) | async-done | bytes 6176 | tf_op jit(solution)/shard_map/all_to_all | solution.py:129
  65.4 3.5 %all-to-all-start.1 = ((f32[3,2,16,16,128]{4,3,0,1,2:T(8,128)}), f32[3,2,16,16,128]{4,3,0,1,2:T(8,128)S(1)}, u32[]{:S(2)}, u32[]{:S(2)}) async-start(f32[3,2,16,16,128]{4,3,0,1,2:T(8,128)} %copy.135), calls=%async_computation.1 | async-start | bytes 1572864 | tf_op jit(solution)/shard_map/all_to_all | solution.py:122
  69.0 0.6 reduce.1
  71.1 0.6 copy.162
  71.7 15.7 %all-to-all-done.1 = f32[3,2,16,16,128]{4,3,0,1,2:T(8,128)S(1)} async-done(((f32[3,2,16,16,128]{4,3,0,1,2:T(8,128)}), f32[3,2,16,16,128]{4,3,0,1,2:T(8,128)S(1)}, u32[]{:S(2)}, u32[]{:S(2)}) %all-to-all-start.1) | async-done | bytes 786464 | tf_op jit(solution)/shard_map/all_to_all | solution.py:122
  87.4 3.5 %all-to-all-start.7 = ((f32[3,2,8,16]{3,1,0,2:T(2,128)}), f32[3,2,8,16]{3,1,0,2:T(2,128)S(1)}, u32[]{:S(2)}, u32[]{:S(2)}) async-start(f32[3,2,8,16]{3,1,0,2:T(2,128)} %copy.162), calls=%async_computation.7 | async-start | bytes 49152 | tf_op jit(solution)/shard_map/all_to_all | solution.py:136
  91.4 1.5 copy.140
  92.9 4.7 %all-to-all-done.7 = f32[3,2,8,16]{3,1,0,2:T(2,128)S(1)} async-done(((f32[3,2,8,16]{3,1,0,2:T(2,128)}), f32[3,2,8,16]{3,1,0,2:T(2,128)S(1)}, u32[]{:S(2)}, u32[]{:S(2)}) %all-to-all-start.7) | async-done | bytes 3104 | tf_op jit(solution)/shard_map/all_to_all | solution.py:136
  97.6 3.5 %all-to-all-start.2 = ((f32[3,2,2,128,128]{4,2,1,0,3:T(2,128)}), f32[3,2,2,128,128]{4,2,1,0,3:T(2,128)S(1)}, u32[]{:S(2)}, u32[]{:S(2)}) async-start(f32[3,2,2,128,128]{4,2,1,0,3:T(2,128)} %copy.140), calls=%async_computation.2 | async-start | bytes 1572864 | tf_op jit(solution)/shard_map/all_to_all | solution.py:128
  101.1 3.8 %collective-permute-start = (f32[4,1,64,128]{3,2,0,1:T(8,128)S(1)}, f32[4,1,64,128]{3,2,0,1:T(8,128)S(1)}, u32[]{:S(2)}, u32[]{:S(2)}) collective-permute-start(f32[4,1,64,128]{3,2,0,1:T(8,128)S(1)} %pad_maximum_fusion.12), channel_id=1, source_target_pairs={{0,2},{2,4},{4,6},{6,8},{8,10},{10,12},{12,14},{1,3},{3,5},{5,7},{... | collective-permute-start | bytes 393224 | tf_op jit(solution)/shard_map/ppermute | solution.py:20
  105.0 1.5 collective-permute-start.1
  107.3 13.6 %all-to-all-done.2 = f32[3,2,2,128,128]{4,2,1,0,3:T(2,128)S(1)} async-done(((f32[3,2,2,128,128]{4,2,1,0,3:T(2,128)}), f32[3,2,2,128,128]{4,2,1,0,3:T(2,128)S(1)}, u32[]{:S(2)}, u32[]{:S(2)}) %all-to-all-start.2) | async-done | bytes 786464 | tf_op jit(solution)/shard_map/all_to_all | solution.py:128
  120.9 0.6 copy.142
  123.0 0.8 copy.143
  123.9 3.5 %all-to-all-start.3 = ((f32[3,2,8,16,128]{4,3,0,1,2:T(8,128)}), f32[3,2,8,16,128]{4,3,0,1,2:T(8,128)S(1)}, u32[]{:S(2)}, u32[]{:S(2)}) async-start(f32[3,2,8,16,128]{4,3,0,1,2:T(8,128)} %copy.143), calls=%async_computation.3 | async-start | bytes 786432 | tf_op jit(solution)/shard_map/all_to_all | solution.py:135
  127.4 0.4 fusion.19
  127.8 0.5 fusion.81
  128.2 0.5 fusion.18
  128.9 0.8 reshape.494
  129.8 0.6 copy-done.5
  130.4 0.7 dynamic-slice
  131.8 7.5 %reduce-scatter.4.cloned.1.call-done = f32[64,6]{1,0:T(8,128)} async-done(((f32[128,6]{1,0:T(8,128)}), f32[64,6]{1,0:T(8,128)}) %reduce-scatter.4.cloned.1.call-update) | async-done | bytes 1552
  139.2 0.9 reshape.495
  140.2 2.1 %collective-permute-start.2 = (f32[4,3,1,128]{3,2,0,1:T(1,128)S(1)}, f32[4,3,1,128]{3,2,0,1:T(1,128)S(1)}, u32[]{:S(2)}, u32[]{:S(2)}) collective-permute-start(f32[4,3,1,128]{3,2,0,1:T(1,128)S(1)} %get-tuple-element.19), channel_id=1, source_target_pairs={{0,1},{2,3},{4,5},{6,7},{8,9},{10,11},{12,13},{14,15},{16,17},{18,... | collective-permute-start | bytes 18440 | tf_op jit(solution)/shard_map/ppermute | solution.py:20
  142.3 1.3 collective-permute-start.3
  143.7 0.6 fusion.38
  144.3 0.6 fusion.39
  145.0 0.6 fusion.3
  145.7 0.6 fusion.2
  146.3 0.9 copy.147
  147.5 20.4 %all-reduce.4.cloned.1.call-done = f32[3,2,128,128]{3,1,0,2:T(2,128)} async-done(((f32[3,2,128,128]{3,1,0,2:T(2,128)}), f32[3,2,128,128]{3,1,0,2:T(2,128)}) %all-reduce.4.cloned.1.call-update) | async-done | bytes 393232
  167.9 1.2 constant_dynamic-slice_fusion
  169.1 1.0 fusion.11
  (95 shorter events, 7.8 us)
Async XLA Ops:
  6.5 0.7 copy-start.4
  7.8 3.5 %copy-start.1 = (f32[3,1,64,128]{3,2,1,0:T(8,128)S(1)}, f32[3,1,64,128]{3,2,1,0:T(8,128)}, u32[]{:S(2)}) copy-start(f32[3,1,64,128]{3,2,1,0:T(8,128)} %param.5) | copy-start | bytes 294916
  8.6 0.8 copy-start.2
  15.6 14.5 %all-to-all-start.4 = ((f32[3,2,1,128]{0,1,2,3:T(2,128)}), f32[3,2,1,128]{0,1,2,3:T(2,128)S(1)}, u32[]{:S(2)}, u32[]{:S(2)}) async-start(f32[3,2,1,128]{0,1,2,3:T(2,128)} %copy.150), calls=%async_computation.4 | async-start | bytes 262144 | tf_op jit(solution)/shard_map/all_to_all | solution.py:116
  32.2 9.8 %all-to-all-start.5 = ((f32[8,1,192]{2,1,0:T(1,128)}), f32[8,1,192]{2,1,0:T(1,128)S(1)}, u32[]{:S(2)}, u32[]{:S(2)}) async-start(f32[8,1,192]{2,1,0:T(1,128)} %reshape.497), calls=%async_computation.5 | async-start | bytes 16384 | tf_op jit(solution)/shard_map/all_to_all | solution.py:123
  36.5 9.0 %copy-start.3 = (f32[6,2,128]{2,1,0:T(2,128)S(1)}, f32[6,2,128]{2,1,0:T(2,128)}, u32[]{:S(2)}) copy-start(f32[6,2,128]{2,1,0:T(2,128)} %param.9) | copy-start | bytes 18436
  42.0 13.2 %all-to-all-start = ((f32[3,2,1,128,128]{4,1,2,0,3:T(2,128)}), f32[3,2,1,128,128]{4,1,2,0,3:T(2,128)S(1)}, u32[]{:S(2)}, u32[]{:S(2)}) async-start(f32[3,2,1,128,128]{4,1,2,0,3:T(2,128)} %copy.131), calls=%async_computation | async-start | bytes 786432 | tf_op jit(solution)/shard_map/all_to_all | solution.py:115
  55.2 10.2 %all-to-all-start.6 = ((f32[8,1,192]{2,1,0:T(1,128)}), f32[8,1,192]{2,1,0:T(1,128)S(1)}, u32[]{:S(2)}, u32[]{:S(2)}) async-start(f32[8,1,192]{2,1,0:T(1,128)} %reshape.499), calls=%async_computation.6 | async-start | bytes 16384 | tf_op jit(solution)/shard_map/all_to_all | solution.py:129
  62.4 6.5 %copy-start = (f32[6,2,128,128]{3,2,1,0:T(8,128)S(1)}, f32[6,2,128,128]{3,2,1,0:T(8,128)}, u32[]{:S(2)}) copy-start(f32[6,2,128,128]{3,2,1,0:T(8,128)} %param.8) | copy-start | bytes 2359300
  65.4 22.0 %all-to-all-start.1 = ((f32[3,2,16,16,128]{4,3,0,1,2:T(8,128)}), f32[3,2,16,16,128]{4,3,0,1,2:T(8,128)S(1)}, u32[]{:S(2)}, u32[]{:S(2)}) async-start(f32[3,2,16,16,128]{4,3,0,1,2:T(8,128)} %copy.135), calls=%async_computation.1 | async-start | bytes 1572864 | tf_op jit(solution)/shard_map/all_to_all | solution.py:122
  87.4 10.2 %all-to-all-start.7 = ((f32[3,2,8,16]{3,1,0,2:T(2,128)}), f32[3,2,8,16]{3,1,0,2:T(2,128)S(1)}, u32[]{:S(2)}, u32[]{:S(2)}) async-start(f32[3,2,8,16]{3,1,0,2:T(2,128)} %copy.162), calls=%async_computation.7 | async-start | bytes 49152 | tf_op jit(solution)/shard_map/all_to_all | solution.py:136
  97.6 23.3 %all-to-all-start.2 = ((f32[3,2,2,128,128]{4,2,1,0,3:T(2,128)}), f32[3,2,2,128,128]{4,2,1,0,3:T(2,128)S(1)}, u32[]{:S(2)}, u32[]{:S(2)}) async-start(f32[3,2,2,128,128]{4,2,1,0,3:T(2,128)} %copy.140), calls=%async_computation.2 | async-start | bytes 1572864 | tf_op jit(solution)/shard_map/all_to_all | solution.py:128
  101.1 39.1 %collective-permute-start = (f32[4,1,64,128]{3,2,0,1:T(8,128)S(1)}, f32[4,1,64,128]{3,2,0,1:T(8,128)S(1)}, u32[]{:S(2)}, u32[]{:S(2)}) collective-permute-start(f32[4,1,64,128]{3,2,0,1:T(8,128)S(1)} %pad_maximum_fusion.12), channel_id=1, source_target_pairs={{0,2},{2,4},{4,6},{6,8},{8,10},{10,12},{12,14},{1,3},{3,5},{5,7},{... | collective-permute-start | bytes 393224 | tf_op jit(solution)/shard_map/ppermute | solution.py:20
  105.0 35.2 %collective-permute-start.1 = (f32[4,1,64,128]{3,2,0,1:T(8,128)S(1)}, f32[4,1,64,128]{3,2,0,1:T(8,128)S(1)}, u32[]{:S(2)}, u32[]{:S(2)}) collective-permute-start(f32[4,1,64,128]{3,2,0,1:T(8,128)S(1)} %pad_maximum_fusion.12), channel_id=1, source_target_pairs={{2,0},{4,2},{6,4},{8,6},{10,8},{12,10},{14,12},{3,1},{5,3},{7,5},{... | collective-permute-start | bytes 393224 | tf_op jit(solution)/shard_map/ppermute | solution.py:22
  123.9 19.8 %all-to-all-start.3 = ((f32[3,2,8,16,128]{4,3,0,1,2:T(8,128)}), f32[3,2,8,16,128]{4,3,0,1,2:T(8,128)S(1)}, u32[]{:S(2)}, u32[]{:S(2)}) async-start(f32[3,2,8,16,128]{4,3,0,1,2:T(8,128)} %copy.143), calls=%async_computation.3 | async-start | bytes 786432 | tf_op jit(solution)/shard_map/all_to_all | solution.py:135
  127.3 11.9 %reduce-scatter.4.cloned.1.call-start = ((), (), s32[]{:S(2)}) async-start(), calls=%async_computation.9 | async-start | bytes 98304
  129.7 38.2 %all-reduce.4.cloned.1.call-start = ((), (), s32[]{:S(2)}) async-start(), calls=%async_computation.10 | async-start | bytes 786432
  129.8 0.7 copy-start.5
  140.2 7.1 %collective-permute-start.2 = (f32[4,3,1,128]{3,2,0,1:T(1,128)S(1)}, f32[4,3,1,128]{3,2,0,1:T(1,128)S(1)}, u32[]{:S(2)}, u32[]{:S(2)}) collective-permute-start(f32[4,3,1,128]{3,2,0,1:T(1,128)S(1)} %get-tuple-element.19), channel_id=1, source_target_pairs={{0,1},{2,3},{4,5},{6,7},{8,9},{10,11},{12,13},{14,15},{16,17},{18,... | collective-permute-start | bytes 18440 | tf_op jit(solution)/shard_map/ppermute | solution.py:20
  142.3 4.9 %collective-permute-start.3 = (f32[4,3,1,128]{3,2,0,1:T(1,128)S(1)}, f32[4,3,1,128]{3,2,0,1:T(1,128)S(1)}, u32[]{:S(2)}, u32[]{:S(2)}) collective-permute-start(f32[4,3,1,128]{3,2,0,1:T(1,128)S(1)} %get-tuple-element.20), channel_id=1, source_target_pairs={{1,0},{3,2},{5,4},{7,6},{9,8},{11,10},{13,12},{15,14},{17,16},{19,... | collective-permute-start | bytes 18440 | tf_op jit(solution)/shard_map/ppermute | solution.py:22
Sparse Core Ops, SparseCore 0:
  130.3 8.8 reduce-scatter.3
  147.4 20.4 all-reduce.3
where the time goes:
time: 178 us; the launch traced here: 177 us
  waiting for transfers between devices  81 us (46%)
  starting transfers between devices  40.5 us (23%)
  local copies, waits for them, and re-layouts  18.3 us (10%)
  matrix products  15.2 us (9%)
  between operations  14.8 us (8%)
  other arithmetic  5.07 us (3%)
  blocking collectives  2.08 us (1%)
    unnamed x4, waiting for transfers between devices  27.9 us
    all_to_all x1, waiting for transfers between devices, local(): lax.all_to_all(done_main, 'gz', split_axis=2, concat_axis=3, tiled=True)  15.7 us
    all_to_all x1, waiting for transfers between devices, local(): lax.all_to_all(field_main, 'gz', split_axis=3, concat_axis=2, tiled=True)  13.6 us
    all_to_all x1, starting transfers between devices, local(): lax.all_to_all(spec_nyq[:, :, None], 'gz', split_axis=3, concat_axis=2, t...  7.15 us
    all_to_all x1, waiting for transfers between devices, local(): lax.all_to_all(spec_main[:, :, None], 'gz', split_axis=3, concat_axis=2,...  7.02 us
    unnamed x25, local copies, waits for them, and re-layouts  6.98 us
    ppermute x2, starting transfers between devices, with_halo(): lax.ppermute(tail, axis, [(i, (i + 1) % count) for i in range(ends)])  5.94 us
    all_to_all x1, waiting for transfers between devices, local(): lax.all_to_all(done_nyq, 'gz', split_axis=2, concat_axis=3, tiled=True)  5.5 us
  transfers between devices with their start and end apart: 14, of which 9 were waited for; matrix products, arithmetic and copies ran while one was open for 15% of the time, Pallas kernels for 0%

commit v1 on v0

--- a/solution.py
+++ b/solution.py
@@ -119,7 +119,12 @@
     done_main = plane_transform(sent_main, cosine, sine, -1.0)
     done_nyq = plane_transform(sent_nyq, cosine, sine, -1.0)
     full_main, full_nyq = (
-        lax.all_to_all(done_main, "gz", split_axis=2, concat_axis=3, tiled=True),
+        jnp.concatenate(
+            lax.all_to_all(
+                jnp.stack(jnp.split(done_main, lax.axis_size("gz"), axis=2)), "gz", 0, 0
+            ),
+            axis=3,
+        ),
         lax.all_to_all(done_nyq, "gz", split_axis=2, concat_axis=3, tiled=True),
     )
     field_main = apply_kernel(full_main, kernel_main)

time: 178 us -> 182 us (1.022)
  other arithmetic: 5.07 us -> 10.4 us
  starting transfers between devices: 40.5 us -> 43 us
  waiting for transfers between devices: 81 us -> 78.8 us
    unnamed x0 -> x7, other arithmetic: none -> 4.7 us
    all_to_all x1, waiting for transfers between devices: 2.94 us -> 0.01 us  [local(): lax.all_to_all(field_nyq, 'gz', split_axis=3, concat_axis=2, tiled=True)]
    all_to_all x1, starting transfers between devices: 3.55 us -> 6.13 us  [local(): lax.all_to_all(jnp.stack(jnp.split(done_main, lax.axis_size('gz'), axis=2...]
  transfers between devices with their start and end apart: 14 -> 14, of which waited for: 9 -> 8; matrix products, arithmetic and copies ran while one was open for 15% -> 17% of each run, Pallas kernels for 0% -> 0%
where the time goes in v1:
time: 182 us; the launch traced here: 181 us
  waiting for transfers between devices  78.8 us (43%)
  starting transfers between devices  43 us (24%)
  local copies, waits for them, and re-layouts  17.1 us (9%)
  matrix products  15.2 us (8%)
  between operations  14.8 us (8%)
  other arithmetic  10.4 us (6%)
  blocking collectives  2.08 us (1%)
    unnamed x4, waiting for transfers between devices  27.9 us
    all_to_all x1, waiting for transfers between devices, local(): lax.all_to_all(jnp.stack(jnp.split(done_main, lax.axis_size('gz'), axis=2...  16 us
    all_to_all x1, waiting for transfers between devices, local(): lax.all_to_all(field_main, 'gz', split_axis=3, concat_axis=2, tiled=True)  13.9 us
    all_to_all x1, starting transfers between devices, local(): lax.all_to_all(spec_nyq[:, :, None], 'gz', split_axis=3, concat_axis=2, t...  7.15 us
    all_to_all x1, waiting for transfers between devices, local(): lax.all_to_all(spec_main[:, :, None], 'gz', split_axis=3, concat_axis=2,...  7.02 us
    unnamed x25, local copies, waits for them, and re-layouts  6.99 us
    all_to_all x1, starting transfers between devices, local(): lax.all_to_all(jnp.stack(jnp.split(done_main, lax.axis_size('gz'), axis=2...  6.13 us
    ppermute x2, starting transfers between devices, with_halo(): lax.ppermute(tail, axis, [(i, (i + 1) % count) for i in range(ends)])  5.93 us
  transfers between devices with their start and end apart: 14, of which 8 were waited for; matrix products, arithmetic and copies ran while one was open for 17% of the time, Pallas kernels for 0%

profile of v1, /device:TPU:0, one launch (start us, length us, event | category | flops | bytes accessed | tf_op | source)
XLA Modules:
  0.0 181.4 jit_solution(17692676030102466235)
XLA Ops:
  6.5 0.6 copy-done.4
  7.2 0.6 fusion.331
  7.8 0.8 broadcast_multiply_fusion.2
  8.7 0.7 copy-done.2
  9.4 1.9 %add_bitcast_fusion = f32[64,128]{1,0:T(8,128)S(1)} fusion(s32[1,64,128]{2,1,0:T(8,128)S(1)} %copy-done.2, f32[]{:T(128)} %bitcast.4, f32[]{:T(128)} %bitcast.3, f32[]{:T(128)} %bitcast.2), kind=kLoop, calls=%fused_computation.200 | loop fusion | flops 65536 | bytes 65548 | tf_op jit(solution)/shard_map/mul | solution.py:106
  11.3 2.1 %all-gather = f32[3,1,128,128]{3,2,0,1:T(8,128)S(1)} all-gather(f32[3,1,64,128]{3,2,0,1:T(8,128)S(1)} %get-tuple-element.28), channel_id=2, replica_groups=mesh['parts'=2,'gz'=8,'gy'=2] {'gy'}, dimensions={2}, use_global_device_ids=true | all-gather | bytes 294912 | tf_op jit(solution)/shard_map/all_gather | solution.py:107
  14.2 0.5 fusion.20
  14.8 0.8 copy.110
  15.6 7.1 %all-to-all-start.4 = ((f32[3,2,1,128]{0,1,2,3:T(2,128)}), f32[3,2,1,128]{0,1,2,3:T(2,128)S(1)}, u32[]{:S(2)}, u32[]{:S(2)}) async-start(f32[3,2,1,128]{0,1,2,3:T(2,128)} %copy.110), calls=%async_computation.4 | async-start | bytes 262144 | tf_op jit(solution)/shard_map/all_to_all | solution.py:116
  23.6 0.7 fusion.36
  24.3 0.7 fusion.37
  25.0 0.7 fusion.7
  25.7 0.7 fusion.6
  26.4 3.7 %all-to-all-done.4 = f32[3,2,1,128]{0,1,2,3:T(2,128)S(1)} async-done(((f32[3,2,1,128]{0,1,2,3:T(2,128)}), f32[3,2,1,128]{0,1,2,3:T(2,128)S(1)}, u32[]{:S(2)}, u32[]{:S(2)}) %all-to-all-start.4) | async-done | bytes 3104 | tf_op jit(solution)/shard_map/all_to_all | solution.py:116
  31.5 0.7 reshape.502
  32.2 3.3 %all-to-all-start.5 = ((f32[8,1,192]{2,1,0:T(1,128)}), f32[8,1,192]{2,1,0:T(1,128)S(1)}, u32[]{:S(2)}, u32[]{:S(2)}) async-start(f32[8,1,192]{2,1,0:T(1,128)} %reshape.502), calls=%async_computation.5 | async-start | bytes 16384 | tf_op jit(solution)/shard_map/all_to_all | solution.py:128
  35.6 0.9 copy.93
  36.5 5.5 %all-to-all-done.5 = f32[8,1,192]{2,1,0:T(1,128)S(1)} async-done(((f32[8,1,192]{2,1,0:T(1,128)}), f32[8,1,192]{2,1,0:T(1,128)S(1)}, u32[]{:S(2)}, u32[]{:S(2)}) %all-to-all-start.5) | async-done | bytes 6176 | tf_op jit(solution)/shard_map/all_to_all | solution.py:128
  42.0 3.5 %all-to-all-start = ((f32[3,2,1,128,128]{4,1,2,0,3:T(2,128)}), f32[3,2,1,128,128]{4,1,2,0,3:T(2,128)S(1)}, u32[]{:S(2)}, u32[]{:S(2)}) async-start(f32[3,2,1,128,128]{4,1,2,0,3:T(2,128)} %copy.93), calls=%async_computation | async-start | bytes 786432 | tf_op jit(solution)/shard_map/all_to_all | solution.py:115
  46.0 0.6 reduce
  47.2 1.0 reshape.504
  48.2 7.0 %all-to-all-done = f32[3,2,1,128,128]{4,1,2,0,3:T(2,128)S(1)} async-done(((f32[3,2,1,128,128]{4,1,2,0,3:T(2,128)}), f32[3,2,1,128,128]{4,1,2,0,3:T(2,128)S(1)}, u32[]{:S(2)}, u32[]{:S(2)}) %all-to-all-start) | async-done | bytes 393248 | tf_op jit(solution)/shard_map/all_to_all | solution.py:115
  55.2 3.7 %all-to-all-start.6 = ((f32[8,1,192]{2,1,0:T(1,128)}), f32[8,1,192]{2,1,0:T(1,128)S(1)}, u32[]{:S(2)}, u32[]{:S(2)}) async-start(f32[8,1,192]{2,1,0:T(1,128)} %reshape.504), calls=%async_computation.6 | async-start | bytes 16384 | tf_op jit(solution)/shard_map/all_to_all | solution.py:134
  58.9 0.6 convolution_multiply_fusion
  59.5 0.6 convolution_multiply_fusion.1
  60.1 0.6 fusion
  60.7 0.6 fusion.1
  61.2 0.7 fusion.51
  61.9 0.7 fusion.54
  62.6 0.7 fusion.57
  63.2 0.7 fusion.60
  63.9 0.7 fusion.63
  64.6 0.7 fusion.66
  65.3 0.7 fusion.48
  65.9 0.7 fusion.69
  66.6 6.1 %all-to-all-start.1 = ((f32[8,3,2,2,16,128]{5,3,4,1,2,0:T(2,128)}), f32[8,3,2,2,16,128]{5,3,4,1,2,0:T(2,128)S(1)}, u32[]{:S(2)}, u32[]{:S(2)}) async-start(f32[8,3,2,2,16,128]{5,3,4,1,2,0:T(2,128)} %fusion.69), calls=%async_computation.1 | async-start | bytes 1572864 | tf_op jit(solution)/shard_map/all_to_all | solution.py:123
  72.8 0.6 reduce.1
  74.9 0.6 copy.122
  75.5 16.0 %all-to-all-done.1 = f32[8,3,2,2,16,128]{5,3,4,1,2,0:T(2,128)S(1)} async-done(((f32[8,3,2,2,16,128]{5,3,4,1,2,0:T(2,128)}), f32[8,3,2,2,16,128]{5,3,4,1,2,0:T(2,128)S(1)}, u32[]{:S(2)}, u32[]{:S(2)}) %all-to-all-start.1) | async-done | bytes 786464 | tf_op jit(solution)/shard_map/all_to_all | solution.py:123
  91.6 3.5 %all-to-all-start.7 = ((f32[3,2,8,16]{3,1,0,2:T(2,128)}), f32[3,2,8,16]{3,1,0,2:T(2,128)S(1)}, u32[]{:S(2)}, u32[]{:S(2)}) async-start(f32[3,2,8,16]{3,1,0,2:T(2,128)} %copy.122), calls=%async_computation.7 | async-start | bytes 49152 | tf_op jit(solution)/shard_map/all_to_all | solution.py:141
  95.5 1.5 copy.100
  97.0 4.8 %all-to-all-done.7 = f32[3,2,8,16]{3,1,0,2:T(2,128)S(1)} async-done(((f32[3,2,8,16]{3,1,0,2:T(2,128)}), f32[3,2,8,16]{3,1,0,2:T(2,128)S(1)}, u32[]{:S(2)}, u32[]{:S(2)}) %all-to-all-start.7) | async-done | bytes 3104 | tf_op jit(solution)/shard_map/all_to_all | solution.py:141
  101.7 3.5 %all-to-all-start.2 = ((f32[3,2,2,128,128]{4,2,1,0,3:T(2,128)}), f32[3,2,2,128,128]{4,2,1,0,3:T(2,128)S(1)}, u32[]{:S(2)}, u32[]{:S(2)}) async-start(f32[3,2,2,128,128]{4,2,1,0,3:T(2,128)} %copy.100), calls=%async_computation.2 | async-start | bytes 1572864 | tf_op jit(solution)/shard_map/all_to_all | solution.py:133
  105.3 3.8 %collective-permute-start = (f32[4,1,64,128]{3,2,0,1:T(8,128)S(1)}, f32[4,1,64,128]{3,2,0,1:T(8,128)S(1)}, u32[]{:S(2)}, u32[]{:S(2)}) collective-permute-start(f32[4,1,64,128]{3,2,0,1:T(8,128)S(1)} %pad_maximum_fusion.11), channel_id=1, source_target_pairs={{0,2},{2,4},{4,6},{6,8},{8,10},{10,12},{12,14},{1,3},{3,5},{5,7},{... | collective-permute-start | bytes 393224 | tf_op jit(solution)/shard_map/ppermute | solution.py:20
  109.1 1.5 collective-permute-start.1
  111.4 13.9 %all-to-all-done.2 = f32[3,2,2,128,128]{4,2,1,0,3:T(2,128)S(1)} async-done(((f32[3,2,2,128,128]{4,2,1,0,3:T(2,128)}), f32[3,2,2,128,128]{4,2,1,0,3:T(2,128)S(1)}, u32[]{:S(2)}, u32[]{:S(2)}) %all-to-all-start.2) | async-done | bytes 786464 | tf_op jit(solution)/shard_map/all_to_all | solution.py:133
  125.4 0.6 copy.102
  127.5 0.8 copy.103
  128.3 3.5 %all-to-all-start.3 = ((f32[3,2,8,16,128]{4,3,0,1,2:T(8,128)}), f32[3,2,8,16,128]{4,3,0,1,2:T(8,128)S(1)}, u32[]{:S(2)}, u32[]{:S(2)}) async-start(f32[3,2,8,16,128]{4,3,0,1,2:T(8,128)} %copy.103), calls=%async_computation.3 | async-start | bytes 786432 | tf_op jit(solution)/shard_map/all_to_all | solution.py:140
  133.3 0.8 reshape.499
  134.2 0.6 copy-done.5
  134.9 0.7 dynamic-slice
  136.2 7.5 %reduce-scatter.4.cloned.1.call-done = f32[64,6]{1,0:T(8,128)} async-done(((f32[128,6]{1,0:T(8,128)}), f32[64,6]{1,0:T(8,128)}) %reduce-scatter.4.cloned.1.call-update) | async-done | bytes 1552
  143.7 0.9 reshape.500
  144.7 2.1 %collective-permute-start.2 = (f32[4,3,1,128]{3,2,0,1:T(1,128)S(1)}, f32[4,3,1,128]{3,2,0,1:T(1,128)S(1)}, u32[]{:S(2)}, u32[]{:S(2)}) collective-permute-start(f32[4,3,1,128]{3,2,0,1:T(1,128)S(1)} %get-tuple-element.19), channel_id=1, source_target_pairs={{0,1},{2,3},{4,5},{6,7},{8,9},{10,11},{12,13},{14,15},{16,17},{18,... | collective-permute-start | bytes 18440 | tf_op jit(solution)/shard_map/ppermute | solution.py:20
  146.8 1.3 collective-permute-start.3
  148.1 0.6 fusion.38
  148.8 0.6 fusion.39
  149.4 0.6 fusion.3
  150.1 0.6 fusion.2
  150.8 0.9 copy.107
  151.9 20.4 %all-reduce.4.cloned.1.call-done = f32[3,2,128,128]{3,1,0,2:T(2,128)} async-done(((f32[3,2,128,128]{3,1,0,2:T(2,128)}), f32[3,2,128,128]{3,1,0,2:T(2,128)}) %all-reduce.4.cloned.1.call-update) | async-done | bytes 393232
  172.3 1.2 constant_dynamic-slice_fusion
  173.6 1.0 fusion.11
  (100 shorter events, 10.5 us)
Async XLA Ops:
  6.5 0.7 copy-start.4
  7.8 3.5 %copy-start.1 = (f32[3,1,64,128]{3,2,1,0:T(8,128)S(1)}, f32[3,1,64,128]{3,2,1,0:T(8,128)}, u32[]{:S(2)}) copy-start(f32[3,1,64,128]{3,2,1,0:T(8,128)} %param.5) | copy-start | bytes 294916
  8.6 0.8 copy-start.2
  15.6 14.5 %all-to-all-start.4 = ((f32[3,2,1,128]{0,1,2,3:T(2,128)}), f32[3,2,1,128]{0,1,2,3:T(2,128)S(1)}, u32[]{:S(2)}, u32[]{:S(2)}) async-start(f32[3,2,1,128]{0,1,2,3:T(2,128)} %copy.110), calls=%async_computation.4 | async-start | bytes 262144 | tf_op jit(solution)/shard_map/all_to_all | solution.py:116
  32.2 9.8 %all-to-all-start.5 = ((f32[8,1,192]{2,1,0:T(1,128)}), f32[8,1,192]{2,1,0:T(1,128)S(1)}, u32[]{:S(2)}, u32[]{:S(2)}) async-start(f32[8,1,192]{2,1,0:T(1,128)} %reshape.502), calls=%async_computation.5 | async-start | bytes 16384 | tf_op jit(solution)/shard_map/all_to_all | solution.py:128
  36.5 9.0 %copy-start.3 = (f32[6,2,128]{2,1,0:T(2,128)S(1)}, f32[6,2,128]{2,1,0:T(2,128)}, u32[]{:S(2)}) copy-start(f32[6,2,128]{2,1,0:T(2,128)} %param.9) | copy-start | bytes 18436
  42.0 13.2 %all-to-all-start = ((f32[3,2,1,128,128]{4,1,2,0,3:T(2,128)}), f32[3,2,1,128,128]{4,1,2,0,3:T(2,128)S(1)}, u32[]{:S(2)}, u32[]{:S(2)}) async-start(f32[3,2,1,128,128]{4,1,2,0,3:T(2,128)} %copy.93), calls=%async_computation | async-start | bytes 786432 | tf_op jit(solution)/shard_map/all_to_all | solution.py:115
  55.2 11.4 %all-to-all-start.6 = ((f32[8,1,192]{2,1,0:T(1,128)}), f32[8,1,192]{2,1,0:T(1,128)S(1)}, u32[]{:S(2)}, u32[]{:S(2)}) async-start(f32[8,1,192]{2,1,0:T(1,128)} %reshape.504), calls=%async_computation.6 | async-start | bytes 16384 | tf_op jit(solution)/shard_map/all_to_all | solution.py:134
  66.6 6.1 %copy-start = (f32[6,2,128,128]{3,2,1,0:T(8,128)S(1)}, f32[6,2,128,128]{3,2,1,0:T(8,128)}, u32[]{:S(2)}) copy-start(f32[6,2,128,128]{3,2,1,0:T(8,128)} %param.8) | copy-start | bytes 2359300
  66.6 24.9 %all-to-all-start.1 = ((f32[8,3,2,2,16,128]{5,3,4,1,2,0:T(2,128)}), f32[8,3,2,2,16,128]{5,3,4,1,2,0:T(2,128)S(1)}, u32[]{:S(2)}, u32[]{:S(2)}) async-start(f32[8,3,2,2,16,128]{5,3,4,1,2,0:T(2,128)} %fusion.69), calls=%async_computation.1 | async-start | bytes 1572864 | tf_op jit(solution)/shard_map/all_to_all | solution.py:123
  91.6 10.2 %all-to-all-start.7 = ((f32[3,2,8,16]{3,1,0,2:T(2,128)}), f32[3,2,8,16]{3,1,0,2:T(2,128)S(1)}, u32[]{:S(2)}, u32[]{:S(2)}) async-start(f32[3,2,8,16]{3,1,0,2:T(2,128)} %copy.122), calls=%async_computation.7 | async-start | bytes 49152 | tf_op jit(solution)/shard_map/all_to_all | solution.py:141
  101.7 23.6 %all-to-all-start.2 = ((f32[3,2,2,128,128]{4,2,1,0,3:T(2,128)}), f32[3,2,2,128,128]{4,2,1,0,3:T(2,128)S(1)}, u32[]{:S(2)}, u32[]{:S(2)}) async-start(f32[3,2,2,128,128]{4,2,1,0,3:T(2,128)} %copy.100), calls=%async_computation.2 | async-start | bytes 1572864 | tf_op jit(solution)/shard_map/all_to_all | solution.py:133
  105.3 39.3 %collective-permute-start = (f32[4,1,64,128]{3,2,0,1:T(8,128)S(1)}, f32[4,1,64,128]{3,2,0,1:T(8,128)S(1)}, u32[]{:S(2)}, u32[]{:S(2)}) collective-permute-start(f32[4,1,64,128]{3,2,0,1:T(8,128)S(1)} %pad_maximum_fusion.11), channel_id=1, source_target_pairs={{0,2},{2,4},{4,6},{6,8},{8,10},{10,12},{12,14},{1,3},{3,5},{5,7},{... | collective-permute-start | bytes 393224 | tf_op jit(solution)/shard_map/ppermute | solution.py:20
  109.1 35.5 %collective-permute-start.1 = (f32[4,1,64,128]{3,2,0,1:T(8,128)S(1)}, f32[4,1,64,128]{3,2,0,1:T(8,128)S(1)}, u32[]{:S(2)}, u32[]{:S(2)}) collective-permute-start(f32[4,1,64,128]{3,2,0,1:T(8,128)S(1)} %pad_maximum_fusion.11), channel_id=1, source_target_pairs={{2,0},{4,2},{6,4},{8,6},{10,8},{12,10},{14,12},{3,1},{5,3},{7,5},{... | collective-permute-start | bytes 393224 | tf_op jit(solution)/shard_map/ppermute | solution.py:22
  128.3 19.8 %all-to-all-start.3 = ((f32[3,2,8,16,128]{4,3,0,1,2:T(8,128)}), f32[3,2,8,16,128]{4,3,0,1,2:T(8,128)S(1)}, u32[]{:S(2)}, u32[]{:S(2)}) async-start(f32[3,2,8,16,128]{4,3,0,1,2:T(8,128)} %copy.103), calls=%async_computation.3 | async-start | bytes 786432 | tf_op jit(solution)/shard_map/all_to_all | solution.py:140
  131.7 11.9 %reduce-scatter.4.cloned.1.call-start = ((), (), s32[]{:S(2)}) async-start(), calls=%async_computation.9 | async-start | bytes 98304
  134.1 38.2 %all-reduce.4.cloned.1.call-start = ((), (), s32[]{:S(2)}) async-start(), calls=%async_computation.10 | async-start | bytes 786432
  134.2 0.7 copy-start.5
  144.7 7.0 %collective-permute-start.2 = (f32[4,3,1,128]{3,2,0,1:T(1,128)S(1)}, f32[4,3,1,128]{3,2,0,1:T(1,128)S(1)}, u32[]{:S(2)}, u32[]{:S(2)}) collective-permute-start(f32[4,3,1,128]{3,2,0,1:T(1,128)S(1)} %get-tuple-element.19), channel_id=1, source_target_pairs={{0,1},{2,3},{4,5},{6,7},{8,9},{10,11},{12,13},{14,15},{16,17},{18,... | collective-permute-start | bytes 18440 | tf_op jit(solution)/shard_map/ppermute | solution.py:20
  146.8 4.9 %collective-permute-start.3 = (f32[4,3,1,128]{3,2,0,1:T(1,128)S(1)}, f32[4,3,1,128]{3,2,0,1:T(1,128)S(1)}, u32[]{:S(2)}, u32[]{:S(2)}) collective-permute-start(f32[4,3,1,128]{3,2,0,1:T(1,128)S(1)} %get-tuple-element.20), channel_id=1, source_target_pairs={{1,0},{3,2},{5,4},{7,6},{9,8},{11,10},{13,12},{15,14},{17,16},{19,... | collective-permute-start | bytes 18440 | tf_op jit(solution)/shard_map/ppermute | solution.py:22
Sparse Core Ops, SparseCore 0:
  134.7 8.8 reduce-scatter.3
  151.8 20.4 all-reduce.3
